TPU v7x, 256 devices: a whole 4x4x8 slice. The times are simulated.
256 devices in a mesh: seq: 32 (over x, z), tensor: 8 (over y, core).
Axes of the slice: x: 4, y: 4, z: 8, core: 2. Of those that a mesh axis runs over, the one named last changes fastest.
Arguments:
- hidden_in: bfloat16 [12288, 4096], P('seq', 'tensor'), may hold values from -6 to 6
- norm_gain: float32 [4096], replicated, may hold values from 0.5 to 1.5
- w_x: bfloat16 [4096, 8192], P('seq', 'tensor'), may hold values from -0.09375 to 0.09375
- w_z: bfloat16 [4096, 8192], P('seq', 'tensor'), may hold values from -0.09375 to 0.09375
- w_bc: bfloat16 [4096, 8, 256], P('seq', 'tensor'), may hold values from -0.09375 to 0.09375
- w_dt: bfloat16 [4096, 64], P('seq', 'tensor'), may hold values from -0.09375 to 0.09375
- dt_bias: float32 [64], P('tensor'), may hold values from -6 to -2
- decay_rate: float32 [64], P('tensor'), may hold values from 8.138021e-05 to 8
- conv_x: float32 [4, 8192], P(None, 'tensor'), may hold values from -3 to 3
- conv_bc: float32 [4, 8, 256], P(None, 'tensor'), may hold values from -3 to 3
- conv_bias_x: float32 [8192], P('tensor'), may hold values from -3 to 3
- conv_bias_bc: float32 [8, 256], P('tensor'), may hold values from -3 to 3
- skip_d: float32 [64], P('tensor'), may hold values from 0.5 to 8
- out_gain: float32 [8192], P('tensor'), may hold values from 0.5 to 1.5
- w_out: bfloat16 [8192, 4096], P('tensor'), may hold values from -0.0625 to 0.0625
Outputs:
- layer_out: bfloat16 [12288, 4096], P('seq', 'tensor')
All inputs are finite; a program needn't handle non-finite values.
Results may differ from a plain program's by a relative error of at most 0.0095.
Values may be sent and summed in bfloat16 or wider, within the bound.
No kernel may reach another device: no remote copies, remote signals or barrier semaphores. Data moves between devices by JAX's collectives and lax.ppermute only.
A program may use at most 128 MiB of HBM per device.

v0:
```python
import functools

import jax
import jax.numpy as jnp
from jax import lax
from jax.experimental import pallas as pl
from jax.experimental.pallas import tpu as pltpu
from jax.sharding import Mesh
from jax.sharding import PartitionSpec as P

SPAN = 128
LEAD = 16
EPS = 1e-05
F32, BF16 = jnp.float32, jnp.bfloat16


def dot(a, b):
    return jnp.dot(a, b, preferred_element_type=F32)


def shifted(block, axis, distance):
    n = lax.axis_size(axis)
    return lax.ppermute(block, axis, [(i, (i + distance) % n) for i in range(n)])


def silu(v):
    return v * jax.nn.sigmoid(v)


def whole(a):
    return pl.BlockSpec(a.shape, lambda s: (0,) * a.ndim)


def each(a):
    return pl.BlockSpec((1, *a.shape[1:]), lambda s: (s,) + (0,) * (a.ndim - 1))


def cost(flops, *arrays):
    moved = sum(a.size * a.dtype.itemsize for a in arrays)
    return pl.CostEstimate(flops=flops, bytes_accessed=moved, transcendentals=0)


def block_copies(blocks, lanes, place_ref, w, sems):
    segments, depth = blocks[0].shape[:2]
    copies = []
    for b, block in enumerate(blocks):
        low = min(lanes, block.shape[2] - w.shape[1])
        for s in range(segments):
            row = pl.multiple_of((s * len(blocks) + place_ref[b]) * depth, depth)
            copies.append(
                pltpu.make_async_copy(
                    block.at[s, :, pl.ds(low, w.shape[1])],
                    w.at[pl.ds(row, depth), :],
                    sems.at[b, s],
                )
            )
    return copies


def proj_kernel(halves, count, place_ref, edge_ref, h_ref, *refs):
    blocks, refs = refs[:count], refs[count:]
    taps_ref, bias_ref, dt_bias_ref, x_ref, bc_ref, dt_ref, w_ref, acc, pre, sems = refs

    @pl.when(pl.program_id(0) == 0)
    def _():
        copies = block_copies(blocks, 0, place_ref, w_ref, sems)
        for copy in copies:
            copy.start()
        for copy in copies:
            copy.wait()

    pieces, feats = h_ref.shape[1], h_ref.shape[3]
    part, total = x_ref.shape[2], pieces * feats
    rows, bc_part = x_ref.shape[1], bc_ref.shape[3] // halves
    lanes = min(128, feats)
    step = pieces // 2
    squares = None
    for j in range(0, pieces, step):
        tall = []
        for i in range(j, j + step):
            h = jnp.concatenate([edge_ref[0, i], h_ref[0, i]], axis=0)
            tall.append(h)
            wide = h.astype(F32)
            for k in range(0, feats, lanes):
                square = wide[:, k : k + lanes] * wide[:, k : k + lanes]
                squares = square if squares is None else squares + square
        product = dot(jnp.concatenate(tall, axis=1), w_ref[j * feats : (j + step) * feats, :])
        if j == 0:
            acc[...] = product
        else:
            acc[...] += product
    scale = lax.rsqrt(jnp.sum(squares, axis=1, keepdims=True) / total + EPS)
    spare = dt_ref.shape[2]
    dt_raw = acc[LEAD:, part:] * scale[LEAD:] + dt_bias_ref[...]
    dt = jnp.maximum(dt_raw, 0.0) + jnp.log1p(jnp.exp(-jnp.abs(dt_raw)))
    lane = lax.broadcasted_iota(jnp.int32, dt.shape, 1)
    dt_ref[0] = jnp.where(lane == spare - 1, scale[LEAD:], dt)
    pre[...] = (acc[...] * scale).astype(BF16).astype(F32)
    taps = taps_ref.shape[0]
    running = bias_ref[...]
    for k in range(taps):
        start = LEAD - taps + 1 + k
        running = running + taps_ref[k : k + 1] * pre[start : start + rows]
    mixed = silu(running).astype(BF16)
    x_ref[0] = mixed[:, :part]
    quarter = mixed[:, part : part + bc_part]
    for side in range(halves):

        @pl.when(lax.rem(pl.program_id(0), halves) == side)
        def _():
            for q in range(bc_ref.shape[0]):
                bc_ref[q, 0, :, side * bc_part : (side + 1) * bc_part] = quarter


def project(place, edge, h, blocks, taps, bias, dt_bias, part, bc_part):
    segments, pieces, rows, feats = h.shape
    low, total = taps.shape[1], pieces * feats
    out = lambda width: pl.BlockSpec((1, rows, width), lambda s, p: (s, 0, 0))
    shape = lambda width, dtype: jax.ShapeDtypeStruct((segments, rows, width), dtype)
    keep = lambda a: pl.BlockSpec(a.shape, lambda s, p: (0,) * a.ndim)
    step = lambda a: pl.BlockSpec((1, *a.shape[1:]), lambda s, p: (s, 0, 0, 0))
    packed = (segments, segments // 2, rows, 2 * bc_part)
    return pl.pallas_call(
        functools.partial(proj_kernel, 2, len(blocks)),
        grid_spec=pltpu.PrefetchScalarGridSpec(
            num_scalar_prefetch=1,
            grid=(segments,),
            in_specs=[
                step(edge),
                step(h),
                *(pl.BlockSpec(memory_space=pl.ANY) for _ in blocks),
                keep(taps),
                keep(bias),
                keep(dt_bias),
            ],
            out_specs=[
                out(part),
                pl.BlockSpec((segments, 1, *packed[2:]), lambda s, p: (0, s // 2, 0, 0)),
                out(low - part),
            ],
            scratch_shapes=[
                pltpu.VMEM((total, low), BF16),
                pltpu.VMEM((rows + LEAD, low), F32),
                pltpu.VMEM((rows + LEAD, low), F32),
                pltpu.SemaphoreType.DMA((len(blocks), segments)),
            ],
        ),
        out_shape=[
            shape(part, BF16),
            jax.ShapeDtypeStruct(packed, BF16),
            shape(low - part, F32),
        ],
        cost_estimate=cost(2 * h.size * low, h),
        name="project",
    )(place, edge, h, *blocks, taps, bias, dt_bias)


def gate_proj_kernel(count, low, place_ref, h_ref, *refs):
    blocks, (dt_ref, z_ref, w_ref, sems) = refs[:count], refs[count:]

    @pl.when(pl.program_id(0) == 0)
    def _():
        copies = block_copies(blocks, low, place_ref, w_ref, sems)
        for copy in copies:
            copy.start()
        for copy in copies:
            copy.wait()

    pieces = h_ref.shape[1]
    tall = jnp.concatenate([h_ref[0, j] for j in range(pieces)], axis=1)
    scale = dt_ref[0, :, dt_ref.shape[2] - 1 :]
    z_ref[0] = (dot(tall, w_ref[...]) * scale).astype(BF16)


def project_gate(place, h, blocks, dt, low, start, count):
    pieces, rows, feats = h.shape[1:]
    part = blocks[0].shape[2] - low
    return pl.pallas_call(
        functools.partial(gate_proj_kernel, len(blocks), low),
        grid_spec=pltpu.PrefetchScalarGridSpec(
            num_scalar_prefetch=1,
            grid=(count,),
            in_specs=[
                pl.BlockSpec((1, pieces, rows, feats), lambda s, p: (s + start, 0, 0, 0)),
                *(pl.BlockSpec(memory_space=pl.ANY) for _ in blocks),
                pl.BlockSpec((1, *dt.shape[1:]), lambda s, p: (s + start, 0, 0)),
            ],
            out_specs=pl.BlockSpec((1, rows, part), lambda s, p: (s, 0, 0)),
            scratch_shapes=[
                pltpu.VMEM((pieces * feats, part), BF16),
                pltpu.SemaphoreType.DMA((len(blocks), blocks[0].shape[0])),
            ],
        ),
        out_shape=jax.ShapeDtypeStruct((count, rows, part), BF16),
        cost_estimate=cost(2 * h.size * part * count // h.shape[0], h),
        name="project_gate",
    )(place, h, *blocks, dt)


def group_rows(quarters_ref, at, first):
    count, width = quarters_ref.shape[0] // 2, quarters_ref.shape[3] // 2
    odd = lax.rem(pl.program_id(0), 2) == 1
    parts = []
    for q in range(count):
        pair = quarters_ref[first * count + q, 0, at]
        parts.append(jnp.where(odd, pair[:, width:], pair[:, :width]))
    return jnp.concatenate(parts, axis=1)


def lower_mask():
    pick = lambda axis: lax.broadcasted_iota(jnp.int32, (SPAN, SPAN), axis)
    return pick(0) >= pick(1)


def decay_kernel(first, head, x_ref, dt_ref, rate_ref, cum_ref, scaled_ref):
    rows, part = x_ref.shape[1:]
    lower = lower_mask().astype(F32)
    for b in range(rows // SPAN):
        at = slice(b * SPAN, (b + 1) * SPAN)
        dt = dt_ref[0, at]
        cum = jnp.dot(
            lower, -dt * rate_ref[...], precision=lax.Precision.HIGHEST, preferred_element_type=F32
        )
        cum_ref[0, at] = cum
        tail = jnp.exp(cum[SPAN - 1 : SPAN] - cum) * dt
        for h in range(part // head):
            cols = slice(h * head, (h + 1) * head)
            wide = x_ref[0, at, cols].astype(F32)
            scaled_ref[0, at, cols] = (wide * tail[:, first + h : first + h + 1]).astype(BF16)


def block_decays(x, dt, rate, first, head):
    return pl.pallas_call(
        functools.partial(decay_kernel, first, head),
        grid=(x.shape[0],),
        in_specs=[each(x), each(dt), whole(rate)],
        out_specs=[each(dt), each(x)],
        out_shape=[
            jax.ShapeDtypeStruct(dt.shape, F32),
            jax.ShapeDtypeStruct(x.shape, BF16),
        ],
        cost_estimate=cost(16 * dt.size * SPAN, x, x, dt, dt),
        name="block_decays",
    )(x, dt, rate)


def states_kernel(first, head, scaled_ref, quarters_ref, cum_ref, enter_ref, message_ref, logs):
    rows, part = scaled_ref.shape[1:]
    segments, chunks = pl.num_programs(0), message_ref.shape[0]
    s = pl.program_id(0)
    base = jnp.zeros_like(cum_ref[0, :1])
    state = None
    for b in range(rows // SPAN):
        at = slice(b * SPAN, (b + 1) * SPAN)
        last = cum_ref[0, (b + 1) * SPAN - 1 : (b + 1) * SPAN]
        base = base + last
        fresh = dot(group_rows(quarters_ref, at, 0).T, scaled_ref[0, at])
        if b:
            enter_ref[0, b - 1] = state
            decay = [
                jnp.broadcast_to(jnp.exp(last[:, first + h : first + h + 1]), (1, head))
                for h in range(part // head)
            ]
            fresh = jnp.concatenate(decay, axis=1) * state + fresh
        state = fresh
    deep = state.shape[0] // chunks
    place = pl.ds(pl.multiple_of(s * deep, deep), deep)
    message_ref[:, place, :] = state.reshape(chunks, deep, part).astype(BF16)
    for h in range(part // head):
        cols = slice(h * head, (h + 1) * head)
        log = jnp.broadcast_to(base[:, first + h : first + h + 1], (1, head))
        high = log.astype(BF16).astype(F32)
        row = lax.broadcasted_iota(jnp.int32, (logs.shape[0], head), 0)
        kept = jnp.where(row == 2 * s + 1, log - high, logs[:, cols])
        logs[:, cols] = jnp.where(row == 2 * s, high, kept)

    @pl.when(s == segments - 1)
    def _():
        tail_rows = logs[...].astype(BF16)
        for q in range(chunks):
            message_ref[q, message_ref.shape[1] - logs.shape[0] :, :] = tail_rows


def quarters_spec(quarters):
    return pl.BlockSpec((quarters.shape[0], 1, *quarters.shape[2:]), lambda s: (0, s // 2, 0, 0))


def block_states(scaled, quarters, cum, first, head, chunks):
    segments, rows, part = scaled.shape
    n = quarters.shape[0] // 2 * quarters.shape[3] // 2
    message = (chunks, segments * n // chunks + 2 * segments, part)
    enter = jax.ShapeDtypeStruct((segments, rows // SPAN - 1, n, part), F32)
    return pl.pallas_call(
        functools.partial(states_kernel, first, head),
        grid=(segments,),
        in_specs=[each(scaled), quarters_spec(quarters), each(cum)],
        out_specs=[each(enter), pl.BlockSpec(message, lambda s: (0, 0, 0))],
        out_shape=[enter, jax.ShapeDtypeStruct(message, BF16)],
        scratch_shapes=[pltpu.VMEM((2 * segments, part), F32)],
        cost_estimate=cost(2 * scaled.size * n, scaled, cum, enter),
        name="block_states",
    )(scaled, quarters, cum)


def intra_kernel(first, head, x_ref, quarters_ref, dt_ref, cum_ref, skip_ref, y_ref, c_ref):
    rows, part = x_ref.shape[1:]
    mask = lower_mask()
    for b in range(rows // SPAN):
        at = slice(b * SPAN, (b + 1) * SPAN)
        cum = cum_ref[0, at]
        cum_rows, dt_rows = cum.T, dt_ref[0, at].T
        c_block = group_rows(quarters_ref, at, 1)
        c_ref[0, at] = c_block
        scores = lax.dot_general(
            c_block,
            group_rows(quarters_ref, at, 0),
            (((1,), (1,)), ((), ())),
            preferred_element_type=F32,
        )
        for h in range(part // head):
            lane = slice(first + h, first + h + 1)
            cols = slice(h * head, (h + 1) * head)
            gap = cum[:, lane] - cum_rows[lane]
            decay = jnp.where(mask, jnp.exp(jnp.where(mask, gap, 0.0)), 0.0)
            mix = (scores * decay * dt_rows[lane]).astype(BF16)
            x = x_ref[0, at, cols]
            y_ref[0, at, cols] = dot(mix, x) + skip_ref[:, cols] * x.astype(F32)


def intra_blocks(x, quarters, dt, cum, skip, first, head):
    segments, rows, _ = x.shape
    n = quarters.shape[0] // 2 * quarters.shape[3] // 2
    return pl.pallas_call(
        functools.partial(intra_kernel, first, head),
        grid=(segments,),
        in_specs=[each(x), quarters_spec(quarters), each(dt), each(cum), whole(skip)],
        out_specs=[each(x), pl.BlockSpec((1, rows, n), lambda s: (s, 0, 0))],
        out_shape=[
            jax.ShapeDtypeStruct(x.shape, F32),
            jax.ShapeDtypeStruct((segments, rows, n), BF16),
        ],
        cost_estimate=cost(64 * x.size * SPAN, x, x, x, dt, cum),
        name="intra_blocks",
    )(x, quarters, dt, cum, skip)


def combine_kernel(segments, r_ref, o_ref):
    places, part = r_ref.shape[0], r_ref.shape[2]
    deep = o_ref.shape[1] // segments
    logs = r_ref[:, segments * deep :, :].astype(F32)
    state = jnp.zeros((deep, part), F32)
    for s in range(segments):
        at = slice(s * deep, (s + 1) * deep)
        for z in range(places):
            o_ref[z, at] = state.astype(BF16)
            decay = jnp.exp(logs[z, 2 * s : 2 * s + 1] + logs[z, 2 * s + 1 : 2 * s + 2])
            state = decay * state + r_ref[z, at].astype(F32)


def combine_states(received, segments):
    places, deep, part = received.shape
    return pl.pallas_call(
        functools.partial(combine_kernel, segments),
        out_shape=jax.ShapeDtypeStruct((places, deep - 2 * segments, part), BF16),
        name="combine_states",
    )(received)


def gate_kernel(first, head, half, y_ref, cum_ref, c_ref, enter_ref, s_ref, z0_ref, z1_ref, o_ref):
    rows, part = y_ref.shape[1:]
    incoming = s_ref[...].reshape(c_ref.shape[2], part).astype(F32)
    base = jnp.zeros_like(cum_ref[0, :1])
    for b in range(rows // SPAN):
        at = slice(b * SPAN, (b + 1) * SPAN)
        cum = cum_ref[0, at]
        for h in range(part // head):
            lane = slice(first + h, first + h + 1)
            cols = slice(h * head, (h + 1) * head)
            enter = incoming[:, cols]
            if b:
                enter = jnp.exp(base[:, lane]) * enter + enter_ref[0, b - 1, :, cols]
            inter = dot(c_ref[0, at], enter.astype(BF16))
            y = y_ref[0, at, cols] + jnp.exp(cum[:, lane]) * inter
            early = pl.program_id(0) < half
            z = jnp.where(early, z0_ref[0, at, cols], z1_ref[0, at, cols]).astype(F32)
            o_ref[0, at, cols] = (y * silu(z)).astype(BF16)
        base = base + cum[SPAN - 1 :]


def gate_blocks(y, cum, c, enter, entering, gates, first, head):
    segments, rows, part = y.shape
    deep = entering.shape[1] // segments
    half = gates[0].shape[0]
    out = jax.ShapeDtypeStruct(y.shape, BF16)
    return pl.pallas_call(
        functools.partial(gate_kernel, first, head, half),
        grid=(segments,),
        in_specs=[
            each(y),
            each(cum),
            each(c),
            each(enter),
            pl.BlockSpec((entering.shape[0], deep, part), lambda s: (0, s, 0)),
            pl.BlockSpec((1, rows, part), lambda s: (jnp.minimum(s, half - 1), 0, 0)),
            pl.BlockSpec((1, rows, part), lambda s: (jnp.maximum(s - half, 0), 0, 0)),
        ],
        out_specs=each(out),
        out_shape=out,
        cost_estimate=cost(2 * y.size * c.shape[2], y, cum, c, enter, out, out),
        name="gate_blocks",
    )(y, cum, c, enter, entering, *gates)


def normed_kernel(at_ref, g_ref, gain_ref, w_ref, first_ref, second_ref, normed_ref):
    quarters, rows, part = g_ref.shape

    @pl.when(pl.program_id(0) == 0)
    def _():
        squares = jnp.zeros((rows, part), F32)
        for q in range(quarters):
            g = g_ref[q].astype(F32)
            squares = squares + g * g
        squares = jnp.sum(squares, axis=1, keepdims=True)
        scale = lax.rsqrt(squares / (quarters * part) + EPS)
        for q in range(quarters):
            cols = slice(q * part, (q + 1) * part)
            normed_ref[:, cols] = (g_ref[q].astype(F32) * scale * gain_ref[:, cols]).astype(BF16)

    for side, o_ref in enumerate((first_ref, second_ref)):

        @pl.when(pl.program_id(0) == side)
        def _():
            o_ref[...] = dot(normed_ref[...], w_ref[...]).astype(BF16)


def out_kernel(at_ref, normed_ref, w_ref, o_ref):
    o_ref[0] = dot(normed_ref[...], w_ref[...]).astype(BF16)


def out_partial(at, targets, inputs, w, rows, width):
    count = len(targets)
    cores = 2
    places = w.shape[1] // (width * cores)

    def tile(i, t):
        distance, other = 0, 0
        for j, (d, o) in enumerate(targets):
            distance = jnp.where(i == j, d, distance)
            other = jnp.where(i == j, o, other)
        return lax.rem(t[0] + distance, places) * cores + jnp.where(other == 1, 1 - t[1], t[1])

    first = len(inputs) > 1
    keep = lambda a: pl.BlockSpec(a.shape, lambda i, t: (0,) * len(a.shape))
    normed = jax.ShapeDtypeStruct((rows, w.shape[0]), BF16)
    one = jax.ShapeDtypeStruct((rows, width), BF16)
    partial = jax.ShapeDtypeStruct((count, rows, width), BF16)
    partial_spec = pl.BlockSpec((1, rows, width), lambda i, t: (i, 0, 0))
    return pl.pallas_call(
        normed_kernel if first else out_kernel,
        grid_spec=pltpu.PrefetchScalarGridSpec(
            num_scalar_prefetch=1,
            grid=(count,),
            in_specs=[
                *(keep(a) for a in inputs),
                pl.BlockSpec((w.shape[0], width), lambda i, t: (0, tile(i, t))),
            ],
            out_specs=[keep(one), keep(one), keep(normed)] if first else partial_spec,
        ),
        out_shape=[one, one, normed] if first else partial,
        cost_estimate=cost(2 * w.shape[0] * rows * width * count, partial, normed),
        name="out_normed" if first else "out_partial",
    )(at, *inputs, w)


def out_shares(gated, gain, w, feats):
    rows = gated.shape[1]
    at = jnp.stack([lax.axis_index("y"), lax.axis_index("c")])
    far_other, far, normed = out_partial(
        at, ((2, 1), (2, 0)), (gated, gain), w, rows, feats
    )
    far_other = shifted(far_other, "c", 1)
    near_other = out_partial(at, ((1, 1), (3, 1), (0, 1)), (normed,), w, rows, feats)
    near_other = shifted(near_other, "c", 1)
    far = (far.astype(F32) + far_other.astype(F32)).astype(BF16)
    upper = shifted(far[: rows // 2], "y", 1)
    lower = shifted(far[rows // 2 :], "y", -1)
    near = out_partial(at, ((1, 0), (3, 0), (0, 0)), (normed,), w, rows, feats)
    blank = jnp.zeros((rows // 2, feats), F32)
    near = [n.astype(F32) + o.astype(F32) for n, o in zip(near, near_other)]
    up = near[0] + jnp.concatenate([upper.astype(F32), blank], axis=0)
    down = near[1] + jnp.concatenate([blank, lower.astype(F32)], axis=0)
    up, down = shifted(up.astype(BF16), "y", 1), shifted(down.astype(BF16), "y", -1)
    return near[2] + up.astype(F32) + down.astype(F32)


def gathered_weights(packed, low, edge):
    nz, zi = lax.axis_size("z"), lax.axis_index("z")
    half = nz // 2
    left = right = packed
    blocks, distances = [packed], [0]
    for step in range(1, half):
        left, right = shifted(left, "z", 1), shifted(right, "z", -1)
        if step == 1:
            left, right, edge = lax.optimization_barrier((left, right, edge))
        blocks += [left, right]
        distances += [-step, step]
    far_low = shifted(left[..., :low], "z", 1)
    far_gate = shifted(right[..., low:], "z", -1)
    place = lax.rem(zi + jnp.array([*distances, half], jnp.int32) + nz, nz)
    peers = lax.axis_size(("x", "y", "c"))
    edges = lax.all_to_all(
        jnp.broadcast_to(edge[None], (peers, *edge.shape)), ("x", "y", "c"), 0, 0, tiled=True
    )
    return place, (*blocks, far_low), (*blocks, far_gate), edges


def local(
    hidden_in,
    norm_gain,
    w_x,
    w_z,
    w_bc,
    w_dt,
    dt_bias,
    decay_rate,
    conv_x,
    conv_bc,
    conv_bias_x,
    conv_bias_bc,
    skip_d,
    out_gain,
    w_out,
):
    nx, nz, ny, nc = (lax.axis_size(a) for a in ("x", "z", "y", "c"))
    xi, zi = (lax.axis_index(a) for a in ("x", "z"))
    rows, feats = hidden_in.shape
    depth, width = w_x.shape
    part = width // nx
    bc_width = w_bc.shape[2]
    bc_part = bc_width // nx
    heads = decay_rate.shape[0]
    own_heads = heads // nx
    taps = conv_x.shape[0]
    low = -(-(part + bc_part + own_heads) // 128) * 128
    spare = low - part - bc_part - own_heads

    gathered = lax.all_gather(hidden_in, ("x", "y", "c"), axis=0)
    gathered = gathered.reshape(nx, ny * nc, rows, feats)
    route = [(i, i + 1) for i in range(nx * nz - 1)]
    edge = lax.ppermute(hidden_in[rows - LEAD :], ("x", "z"), route)

    gain = lax.dynamic_slice(norm_gain, ((xi * nz + zi) * depth,), (depth,))
    pieces = [w.reshape(depth, nx, -1) for w in (w_x, w_bc, w_dt)]
    pieces.append(jnp.zeros((depth, nx, spare), BF16))
    pieces.append(w_z.reshape(depth, nx, part))
    packed = jnp.concatenate(pieces, axis=2).astype(F32) * gain[:, None, None]
    packed = jnp.transpose(packed.astype(BF16), (1, 0, 2))
    packed = lax.all_to_all(packed, "x", 0, 0, tiled=True)
    place, w_low, w_gate, edges = lax.optimization_barrier(gathered_weights(packed, low, edge))
    edges = edges.reshape(nx, ny * nc, LEAD, feats)

    def own(a):
        size = a.shape[-1] // nx
        return lax.dynamic_slice_in_dim(a, xi * size, size, axis=a.ndim - 1)

    row = lambda a: a.reshape(1, -1)
    tap_rows = jnp.concatenate([own(conv_x), own(conv_bc.reshape(taps, -1))], axis=1)
    tap_rows = jnp.pad(tap_rows, ((0, 0), (0, own_heads + spare)))
    bias_row = jnp.concatenate([own(conv_bias_x), own(conv_bias_bc.reshape(-1))])
    bias_row = row(jnp.pad(bias_row, (0, own_heads + spare)))
    in_lanes = lambda a: row(jnp.pad(own(a), (bc_part, spare)))
    x_conv, quarter, dt = project(
        place, edges, gathered, w_low, tap_rows, bias_row, in_lanes(dt_bias), part, bc_part
    )
    head = width // heads
    half = nx // 2
    quarters, (cum, scaled), early_gate = lax.optimization_barrier(
        (
            lax.all_to_all(quarter, "x", 0, 0, tiled=True),
            block_decays(x_conv, dt, in_lanes(decay_rate), bc_part, head),
            project_gate(place, gathered, w_gate, dt, low, 0, half),
        )
    )
    skip_row = row(jnp.repeat(own(skip_d), head))
    enter, message = block_states(scaled, quarters, cum, bc_part, head, nz)
    received, (y, c_rows) = lax.optimization_barrier(
        (
            lax.all_to_all(message, "z", 0, 0, tiled=True),
            intra_blocks(x_conv, quarters, dt, cum, skip_row, bc_part, head),
        )
    )
    states = combine_states(received, nx)
    states, gate_inputs = lax.optimization_barrier((states, gathered))
    entering, late_gate = lax.optimization_barrier(
        (
            lax.all_to_all(states, "z", 0, 0, tiled=True),
            project_gate(place, gate_inputs, w_gate, dt, low, half, nx - half),
        )
    )
    gates = (early_gate, late_gate)
    gated = gate_blocks(y, cum, c_rows, enter, entering, gates, bc_part, head)
    gated = lax.all_to_all(gated, "x", 0, 0, tiled=True)

    summed = out_shares(gated, row(out_gain), w_out, feats)
    return (hidden_in.astype(F32) + summed).astype(BF16)


def solution(mesh):
    sizes = mesh.shape
    devices = mesh.devices.reshape(4, sizes["seq"] // 4, sizes["tensor"] // 2, 2)
    split = Mesh(devices, ("x", "z", "y", "c"))
    seq, tensor = ("x", "z"), ("y", "c")
    in_specs = (
        P(seq, tensor),
        P(),
        P(seq, tensor),
        P(seq, tensor),
        P(seq, tensor, None),
        P(seq, tensor),
        P(tensor),
        P(tensor),
        P(None, tensor),
        P(None, tensor, None),
        P(tensor),
        P(tensor, None),
        P(tensor),
        P(tensor),
        P(tensor, None),
    )
    return jax.shard_map(
        local, mesh=split, in_specs=in_specs, out_specs=P(seq, tensor), check_vma=False
    )
```

profile of v0, /device:TPU:1, one launch (start us, length us, event | category | flops | bytes accessed | tf_op | source)
XLA Modules:
  0.0 224.5 jit_solution(7257435454272673184)
XLA Ops:
  10.8 14.6 %all_to_all.30.refs_0_ = bf16[4,128,640]{2,1,0:T(8,128)(2,1)S(1)} all-to-all(bf16[4,128,640]{2,1,0:T(8,128)(2,1)S(1)} %fusion.5), channel_id=1, replica_groups=mesh['x'=4,'z'=8,'y'=4,'c'=2] {'x'}, dimensions={0} | all-to-all | bytes 1310720 | tf_op jit(solution)/shard_map/all_to_all | solution.py:558
  27.1 3.9 %collective-permute-start.1 = (bf16[4,128,640]{2,1,0:T(8,128)(2,1)S(1)}, bf16[4,128,640]{2,1,0:T(8,128)(2,1)S(1)}, u32[]{:S(2)}, u32[]{:S(2)}) collective-permute-start(bf16[4,128,640]{2,1,0:T(8,128)(2,1)S(1)} %all_to_all.30.refs_0_), channel_id=1, source_target_pairs={{0,56},{8,0},{16,8},{24,16},{32,24},{40,32},{48,40},{56,48},{1,57}... | collective-permute-start | bytes 1966088 | tf_op jit(solution)/shard_map/ppermute | solution.py:23
  33.0 6.7 %collective-permute-done.2 = bf16[16,512]{1,0:T(8,128)(2,1)S(1)} collective-permute-done((bf16[16,512]{1,0:T(8,128)(2,1)S(1)}, bf16[16,512]{1,0:T(8,128)(2,1)S(1)}, u32[]{:S(2)}, u32[]{:S(2)}) %collective-permute-start.2) | collective-permute-done | bytes 16416 | tf_op jit(solution)/shard_map/ppermute | solution.py:550
  39.7 4.6 %collective-permute-done.refs_1_ = bf16[4,128,640]{2,1,0:T(8,128)(2,1)S(1)} collective-permute-done((bf16[4,128,640]{2,1,0:T(8,128)(2,1)S(1)}, bf16[4,128,640]{2,1,0:T(8,128)(2,1)S(1)}, u32[]{:S(2)}, u32[]{:S(2)}) %collective-permute-start) | collective-permute-done | bytes 655392 | tf_op jit(solution)/shard_map/ppermute | solution.py:23
  47.1 12.4 %collective-permute-done.3.refs_3_ = bf16[4,128,640]{2,1,0:T(8,128)(2,1)} collective-permute-done((bf16[4,128,640]{2,1,0:T(8,128)(2,1)S(1)}, bf16[4,128,640]{2,1,0:T(8,128)(2,1)}, u32[]{:S(2)}, u32[]{:S(2)}) %collective-permute-start.3) | collective-permute-done | bytes 655392 | tf_op jit(solution)/shard_map/ppermute | solution.py:23
  64.5 10.4 %all-to-all-start.1 = ((bf16[32,16,512]{2,1,0:T(8,128)(2,1)}), bf16[32,16,512]{2,1,0:T(8,128)(2,1)}, u32[]{:S(2)}, u32[]{:S(2)}) async-start(bf16[32,16,512]{2,1,0:T(8,128)(2,1)} %broadcast_in_dim.7), calls=%async_computation.1 | async-start | bytes 1048576 | tf_op jit(solution)/shard_map/all_to_all | solution.py:511
  80.5 6.6 %all-to-all-done.1 = bf16[32,16,512]{2,1,0:T(8,128)(2,1)} async-done(((bf16[32,16,512]{2,1,0:T(8,128)(2,1)}), bf16[32,16,512]{2,1,0:T(8,128)(2,1)}, u32[]{:S(2)}, u32[]{:S(2)}) %all-to-all-start.1) | async-done | bytes 524320 | tf_op jit(solution)/shard_map/all_to_all | solution.py:511
  87.2 16.0 %project.1 = (bf16[4,384,256]{2,1,0:T(8,128)(2,1)}, bf16[4,2,384,128]{3,2,1,0:T(8,128)(2,1)}, f32[4,384,128]{2,1,0:T(8,128)}) custom-call(s32[8]{0:T(128)} %compare_select_fusion.place_ref, bf16[4,8,16,512]{3,2,1,0:T(8,128)(2,1)} %bitcast.7.edge_ref, bf16[4,8,384,512]{3,2,1,0:T(8,128)(2,1)} %bitcast.35, bf16[4,128,640]{2,1,0:T(8,128)(2,1)} %copy-done.1, ...), custom_call_target="tpu_custom_call" | custom-call | flops 4831838208 | bytes 12582912 | tf_op jit(solution)/shard_map/project/pallas_call | solution.py:123
  103.2 3.7 %all-to-all-start.2 = ((bf16[4,2,384,128]{3,2,1,0:T(8,128)(2,1)}), bf16[4,2,384,128]{3,2,1,0:T(8,128)(2,1)S(1)}, u32[]{:S(2)}, u32[]{:S(2)}) async-start(bf16[4,2,384,128]{3,2,1,0:T(8,128)(2,1)} %get-tuple-element.62), calls=%async_computation.2 | async-start | bytes 1572864 | tf_op jit(solution)/shard_map/all_to_all | solution.py:579
  107.5 4.4 %block_decays.1 = (f32[4,384,128]{2,1,0:T(8,128)}, bf16[4,384,256]{2,1,0:T(8,128)(2,1)}) custom-call(bf16[4,384,256]{2,1,0:T(8,128)(2,1)} %get-tuple-element.63.x_ref, f32[4,384,128]{2,1,0:T(8,128)} %get-tuple-element.64.dt_ref.refs_8_, f32[1,128]{1,0:T(1,128)} %pad_bitcast_fusion.rate_ref), custom_call_target="tpu_custom_call" | custom-call | flops 402653184 | bytes 3145728 | tf_op jit(solution)/shard_map/block_decays/pallas_call | solution.py:233
  111.9 7.3 %project_gate.2.z0_ref = bf16[2,384,256]{2,1,0:T(8,128)(2,1)} custom-call(s32[8]{0:T(128)} %compare_select_fusion.place_ref, bf16[4,8,384,512]{3,2,1,0:T(8,128)(2,1)} %bitcast.36, bf16[4,128,640]{2,1,0:T(8,128)(2,1)} %copy-done.1, bf16[4,128,640]{2,1,0:T(8,128)(2,1)} %copy-done.4, bf16[4,128,640]{2,1,0:T(8,128)(2,1)} %copy-done.5, ...), custom_call_target="tpu_custom_call" | custom-call | flops 1610612736 | bytes 12582912 | tf_op jit(solution)/shard_map/project_gate/pallas_call | solution.py:178
  120.0 4.5 %block_states.1 = (f32[4,2,128,256]{3,2,1,0:T(8,128)}, bf16[8,72,256]{2,1,0:T(8,128)(2,1)}) custom-call(bf16[4,384,256]{2,1,0:T(8,128)(2,1)} %get-tuple-element.75.scaled_ref, bf16[4,2,384,128]{3,2,1,0:T(8,128)(2,1)} %copy-done.7, f32[4,384,128]{2,1,0:T(8,128)} %get-tuple-element.77.cum_ref), custom_call_target="tpu_custom_call" | custom-call | flops 100663296 | bytes 2621440 | tf_op jit(solution)/shard_map/block_states/pallas_call | solution.py:293
  124.5 6.7 %all-to-all-start.3 = ((bf16[8,72,256]{2,1,0:T(8,128)(2,1)}), bf16[8,72,256]{2,1,0:T(8,128)(2,1)S(1)}, u32[]{:S(2)}, u32[]{:S(2)}) async-start(bf16[8,72,256]{2,1,0:T(8,128)(2,1)} %get-tuple-element.78), calls=%async_computation.3 | async-start | bytes 589824 | tf_op jit(solution)/shard_map/all_to_all | solution.py:588
  132.0 6.1 %intra_blocks.1 = (f32[4,384,256]{2,1,0:T(8,128)}, bf16[4,384,128]{2,1,0:T(8,128)(2,1)}) custom-call(bf16[4,384,256]{2,1,0:T(8,128)(2,1)} %get-tuple-element.63.x_ref, bf16[4,2,384,128]{3,2,1,0:T(8,128)(2,1)} %copy-done.7, f32[4,384,128]{2,1,0:T(8,128)} %get-tuple-element.64.dt_ref.refs_8_, f32[4,384,128]{2,1,0:T(8,128)} %get-tuple-element.77.cum_ref, ...), custom_call_target="tpu_custom_call" | custom-call | flops 3221225472 | bytes 3932160 | tf_op jit(solution)/shard_map/intra_blocks/pallas_call | solution.py:333
  138.1 4.4 %all-to-all-done.3.r_ref = bf16[8,72,256]{2,1,0:T(8,128)(2,1)S(1)} async-done(((bf16[8,72,256]{2,1,0:T(8,128)(2,1)}), bf16[8,72,256]{2,1,0:T(8,128)(2,1)S(1)}, u32[]{:S(2)}, u32[]{:S(2)}) %all-to-all-start.3) | async-done | bytes 294944 | tf_op jit(solution)/shard_map/all_to_all | solution.py:588
  148.4 7.3 %project_gate.3.z1_ref = bf16[2,384,256]{2,1,0:T(8,128)(2,1)} custom-call(s32[8]{0:T(128)} %compare_select_fusion.place_ref, bf16[4,8,384,512]{3,2,1,0:T(8,128)(2,1)} %bitcast.37, bf16[4,128,640]{2,1,0:T(8,128)(2,1)} %copy-done.1, bf16[4,128,640]{2,1,0:T(8,128)(2,1)} %copy-done.4, bf16[4,128,640]{2,1,0:T(8,128)(2,1)} %copy-done.5, ...), custom_call_target="tpu_custom_call" | custom-call | flops 1610612736 | bytes 12582912 | tf_op jit(solution)/shard_map/project_gate/pallas_call | solution.py:178
  158.5 4.6 %gate_blocks.1 = bf16[4,384,256]{2,1,0:T(8,128)(2,1)} custom-call(f32[4,384,256]{2,1,0:T(8,128)} %get-tuple-element.81.y_ref, f32[4,384,128]{2,1,0:T(8,128)} %get-tuple-element.77.cum_ref, bf16[4,384,128]{2,1,0:T(8,128)(2,1)} %get-tuple-element.82.c_ref, f32[4,2,128,256]{3,2,1,0:T(8,128)} %get-tuple-element.83.enter_ref, bf16[8,64,256]{2,1,0:T(8,128)(2,1)} %copy-done.11, ...), custom_call_target="tpu_custom_call" | custom-call | flops 100663296 | bytes 5373952 | tf_op jit(solution)/shard_map/gate_blocks/pallas_call | solution.py:395
  163.1 4.1 %all-to-all-start.5 = ((bf16[4,384,256]{2,1,0:T(8,128)(2,1)}), bf16[4,384,256]{2,1,0:T(8,128)(2,1)S(1)}, u32[]{:S(2)}, u32[]{:S(2)}) async-start(bf16[4,384,256]{2,1,0:T(8,128)(2,1)} %gate_blocks.1), calls=%async_computation.5 | async-start | bytes 1572864 | tf_op jit(solution)/shard_map/all_to_all | solution.py:602
  167.8 8.0 %all-to-all-done.5.g_ref = bf16[4,384,256]{2,1,0:T(8,128)(2,1)S(1)} async-done(((bf16[4,384,256]{2,1,0:T(8,128)(2,1)}), bf16[4,384,256]{2,1,0:T(8,128)(2,1)S(1)}, u32[]{:S(2)}, u32[]{:S(2)}) %all-to-all-start.5) | async-done | bytes 786464 | tf_op jit(solution)/shard_map/all_to_all | solution.py:602
  176.7 4.6 %out_normed.1 = (bf16[384,512]{1,0:T(8,128)(2,1)}, bf16[384,512]{1,0:T(8,128)(2,1)}, bf16[384,1024]{1,0:T(8,128)(2,1)}) custom-call(s32[2]{0:T(128)} %pad_add_fusion.at_ref, bf16[4,384,256]{2,1,0:T(8,128)(2,1)} %copy-done.6, f32[1,1024]{1,0:T(1,128)} %bitcast.42, bf16[1024,4096]{1,0:T(8,128)(2,1)} %w_ref.5), custom_call_target="tpu_custom_call" | custom-call | flops 805306368 | bytes 1572864 | tf_op jit(solution)/shard_map/out_normed/pallas_call | solution.py:458
  181.3 5.6 %out_partial.3 = bf16[3,384,512]{2,1,0:T(8,128)(2,1)} custom-call(s32[2]{0:T(128)} %pad_add_fusion.at_ref, bf16[384,1024]{1,0:T(8,128)(2,1)} %get-tuple-element.90.normed_ref, bf16[1024,4096]{1,0:T(8,128)(2,1)} %w_ref.5), custom_call_target="tpu_custom_call" | custom-call | flops 1207959552 | bytes 1966080 | tf_op jit(solution)/shard_map/out_partial/pallas_call | solution.py:458
  186.9 4.7 %collective-permute-start.9 = (bf16[3,384,512]{2,1,0:T(8,128)(2,1)}, bf16[3,384,512]{2,1,0:T(8,128)(2,1)S(1)}, u32[]{:S(2)}, u32[]{:S(2)}) collective-permute-start(bf16[3,384,512]{2,1,0:T(8,128)(2,1)} %out_partial.3), channel_id=1, source_target_pairs={{0,1},{1,0},{2,3},{3,2},{4,5},{5,4},{6,7},{7,6},{8,9},{9,8},{10,11... | collective-permute-start | bytes 3538952 | tf_op jit(solution)/shard_map/ppermute | solution.py:23
  197.7 5.4 %out_partial.2 = bf16[3,384,512]{2,1,0:T(8,128)(2,1)} custom-call(s32[2]{0:T(128)} %pad_add_fusion.at_ref, bf16[384,1024]{1,0:T(8,128)(2,1)} %get-tuple-element.90.normed_ref, bf16[1024,4096]{1,0:T(8,128)(2,1)} %w_ref.5), custom_call_target="tpu_custom_call" | custom-call | flops 1207959552 | bytes 1966080 | tf_op jit(solution)/shard_map/out_partial/pallas_call | solution.py:458
  207.4 8.3 %collective-permute-done.12 = bf16[384,512]{1,0:T(8,128)(2,1)S(1)} collective-permute-done((bf16[384,512]{1,0:T(8,128)(2,1)S(1)}, bf16[384,512]{1,0:T(8,128)(2,1)S(1)}, u32[]{:S(2)}, u32[]{:S(2)}) %collective-permute-start.12) | collective-permute-done | bytes 393248 | tf_op jit(solution)/shard_map/ppermute | solution.py:23
  (111 shorter events, 45.9 us)
Async XLA Ops:
  6.5 56.5 %copy-start = (f32[4,1024]{1,0:T(4,128)S(1)}, f32[4,1024]{1,0:T(4,128)}, u32[]{:S(2)}) copy-start(f32[4,1024]{1,0:T(4,128)} %param.24) | copy-start | bytes 49156
  6.5 80.6 %all-gather.3.cloned.1.call-start = ((), (), s32[]{:S(2)}) async-start(), calls=%async_computation.6 | async-start | bytes 12976128 | tf_op jit(solution)/shard_map/all_gather | solution.py:547
  10.6 52.4 %copy-start.16 = (f32[4,1,256]{2,1,0:T(1,128)S(1)}, f32[4,1,256]{2,1,0:T(1,128)}, u32[]{:S(2)}) copy-start(f32[4,1,256]{2,1,0:T(1,128)} %param.25) | copy-start | bytes 12292
  10.7 64.1 %copy-start.18 = (f32[1,256]{1,0:T(1,128)S(1)}, f32[1,256]{1,0:T(1,128)}, u32[]{:S(2)}) copy-start(f32[1,256]{1,0:T(1,128)} %param.27) | copy-start | bytes 3076
  25.4 18.9 %collective-permute-start = (bf16[4,128,640]{2,1,0:T(8,128)(2,1)S(1)}, bf16[4,128,640]{2,1,0:T(8,128)(2,1)S(1)}, u32[]{:S(2)}, u32[]{:S(2)}) collective-permute-start(bf16[4,128,640]{2,1,0:T(8,128)(2,1)S(1)} %all_to_all.30.refs_0_), channel_id=1, source_target_pairs={{0,8},{8,16},{16,24},{24,32},{32,40},{40,48},{48,56},{56,0},{1,9},... | collective-permute-start | bytes 1966088 | tf_op jit(solution)/shard_map/ppermute | solution.py:23
  27.1 17.2 %collective-permute-start.1 = (bf16[4,128,640]{2,1,0:T(8,128)(2,1)S(1)}, bf16[4,128,640]{2,1,0:T(8,128)(2,1)S(1)}, u32[]{:S(2)}, u32[]{:S(2)}) collective-permute-start(bf16[4,128,640]{2,1,0:T(8,128)(2,1)S(1)} %all_to_all.30.refs_0_), channel_id=1, source_target_pairs={{0,56},{8,0},{16,8},{24,16},{32,24},{40,32},{48,40},{56,48},{1,57}... | collective-permute-start | bytes 1966088 | tf_op jit(solution)/shard_map/ppermute | solution.py:23
  31.7 8.0 %collective-permute-start.2 = (bf16[16,512]{1,0:T(8,128)(2,1)S(1)}, bf16[16,512]{1,0:T(8,128)(2,1)S(1)}, u32[]{:S(2)}, u32[]{:S(2)}) collective-permute-start(bf16[16,512]{1,0:T(8,128)(2,1)S(1)} %slice.15), channel_id=1, source_target_pairs={{0,8},{8,16},{16,24},{24,32},{32,40},{40,48},{48,56},{56,64},{64,7... | collective-permute-start | bytes 49160 | tf_op jit(solution)/shard_map/ppermute | solution.py:550
  44.3 15.1 %collective-permute-start.3 = (bf16[4,128,640]{2,1,0:T(8,128)(2,1)S(1)}, bf16[4,128,640]{2,1,0:T(8,128)(2,1)}, u32[]{:S(2)}, u32[]{:S(2)}) collective-permute-start(bf16[4,128,640]{2,1,0:T(8,128)(2,1)S(1)} %collective-permute-done.refs_1_), channel_id=1, source_target_pairs={{0,8},{8,16},{16,24},{24,32},{32,40},{40,48},{48,56},{56,0},{1,9},... | collective-permute-start | bytes 1966088 | tf_op jit(solution)/shard_map/ppermute | solution.py:23
  44.4 15.0 %collective-permute-start.4 = (bf16[4,128,640]{2,1,0:T(8,128)(2,1)S(1)}, bf16[4,128,640]{2,1,0:T(8,128)(2,1)}, u32[]{:S(2)}, u32[]{:S(2)}) collective-permute-start(bf16[4,128,640]{2,1,0:T(8,128)(2,1)S(1)} %collective-permute-done.1.refs_2_), channel_id=1, source_target_pairs={{0,56},{8,0},{16,8},{24,16},{32,24},{40,32},{48,40},{56,48},{1,57}... | collective-permute-start | bytes 1966088 | tf_op jit(solution)/shard_map/ppermute | solution.py:23
  59.4 15.5 %collective-permute-start.5 = (bf16[4,128,640]{2,1,0:T(8,128)(2,1)}, bf16[4,128,640]{2,1,0:T(8,128)(2,1)S(1)}, u32[]{:S(2)}, u32[]{:S(2)}) collective-permute-start(bf16[4,128,640]{2,1,0:T(8,128)(2,1)} %collective-permute-done.3.refs_3_), channel_id=1, source_target_pairs={{0,8},{8,16},{16,24},{24,32},{32,40},{40,48},{48,56},{56,0},{1,9},... | collective-permute-start | bytes 1966088 | tf_op jit(solution)/shard_map/ppermute | solution.py:23
  59.4 16.5 %collective-permute-start.6 = (bf16[4,128,640]{2,1,0:T(8,128)(2,1)}, bf16[4,128,640]{2,1,0:T(8,128)(2,1)S(1)}, u32[]{:S(2)}, u32[]{:S(2)}) collective-permute-start(bf16[4,128,640]{2,1,0:T(8,128)(2,1)} %collective-permute-done.4.refs_4_), channel_id=1, source_target_pairs={{0,56},{8,0},{16,8},{24,16},{32,24},{40,32},{48,40},{56,48},{1,57}... | collective-permute-start | bytes 1966088 | tf_op jit(solution)/shard_map/ppermute | solution.py:23
  64.5 22.6 %all-to-all-start.1 = ((bf16[32,16,512]{2,1,0:T(8,128)(2,1)}), bf16[32,16,512]{2,1,0:T(8,128)(2,1)}, u32[]{:S(2)}, u32[]{:S(2)}) async-start(bf16[32,16,512]{2,1,0:T(8,128)(2,1)} %broadcast_in_dim.7), calls=%async_computation.1 | async-start | bytes 1048576 | tf_op jit(solution)/shard_map/all_to_all | solution.py:511
  75.8 11.3 %collective-permute-start.7 = (bf16[4,128,384]{2,1,0:T(8,128)(2,1)}, bf16[4,128,384]{2,1,0:T(8,128)(2,1)}, u32[]{:S(2)}, u32[]{:S(2)}) collective-permute-start(bf16[4,128,384]{2,1,0:T(8,128)(2,1)} %slice.20), channel_id=1, source_target_pairs={{0,8},{8,16},{16,24},{24,32},{32,40},{40,48},{48,56},{56,0},{1,9},... | collective-permute-start | bytes 1179656 | tf_op jit(solution)/shard_map/ppermute | solution.py:23
  76.0 11.2 %collective-permute-start.8 = (bf16[4,128,256]{2,1,0:T(8,128)(2,1)S(1)}, bf16[4,128,256]{2,1,0:T(8,128)(2,1)S(1)}, u32[]{:S(2)}, u32[]{:S(2)}) collective-permute-start(bf16[4,128,256]{2,1,0:T(8,128)(2,1)S(1)} %slice.21), channel_id=1, source_target_pairs={{0,56},{8,0},{16,8},{24,16},{32,24},{40,32},{48,40},{56,48},{1,57}... | collective-permute-start | bytes 786440 | tf_op jit(solution)/shard_map/ppermute | solution.py:23
  103.2 16.0 %all-to-all-start.2 = ((bf16[4,2,384,128]{3,2,1,0:T(8,128)(2,1)}), bf16[4,2,384,128]{3,2,1,0:T(8,128)(2,1)S(1)}, u32[]{:S(2)}, u32[]{:S(2)}) async-start(bf16[4,2,384,128]{3,2,1,0:T(8,128)(2,1)} %get-tuple-element.62), calls=%async_computation.2 | async-start | bytes 1572864 | tf_op jit(solution)/shard_map/all_to_all | solution.py:579
  124.5 18.0 %all-to-all-start.3 = ((bf16[8,72,256]{2,1,0:T(8,128)(2,1)}), bf16[8,72,256]{2,1,0:T(8,128)(2,1)S(1)}, u32[]{:S(2)}, u32[]{:S(2)}) async-start(bf16[8,72,256]{2,1,0:T(8,128)(2,1)} %get-tuple-element.78), calls=%async_computation.3 | async-start | bytes 589824 | tf_op jit(solution)/shard_map/all_to_all | solution.py:588
  145.0 12.8 %all-to-all-start.4 = ((bf16[8,64,256]{2,1,0:T(8,128)(2,1)}), bf16[8,64,256]{2,1,0:T(8,128)(2,1)S(1)}, u32[]{:S(2)}, u32[]{:S(2)}) async-start(bf16[8,64,256]{2,1,0:T(8,128)(2,1)} %combine_states.1), calls=%async_computation.4 | async-start | bytes 524288 | tf_op jit(solution)/shard_map/all_to_all | solution.py:596
  163.1 12.6 %all-to-all-start.5 = ((bf16[4,384,256]{2,1,0:T(8,128)(2,1)}), bf16[4,384,256]{2,1,0:T(8,128)(2,1)S(1)}, u32[]{:S(2)}, u32[]{:S(2)}) async-start(bf16[4,384,256]{2,1,0:T(8,128)(2,1)} %gate_blocks.1), calls=%async_computation.5 | async-start | bytes 1572864 | tf_op jit(solution)/shard_map/all_to_all | solution.py:602
  186.9 16.3 %collective-permute-start.9 = (bf16[3,384,512]{2,1,0:T(8,128)(2,1)}, bf16[3,384,512]{2,1,0:T(8,128)(2,1)S(1)}, u32[]{:S(2)}, u32[]{:S(2)}) collective-permute-start(bf16[3,384,512]{2,1,0:T(8,128)(2,1)} %out_partial.3), channel_id=1, source_target_pairs={{0,1},{1,0},{2,3},{3,2},{4,5},{5,4},{6,7},{7,6},{8,9},{9,8},{10,11... | collective-permute-start | bytes 3538952 | tf_op jit(solution)/shard_map/ppermute | solution.py:23
  191.6 3.2 %collective-permute-start.10 = (bf16[384,512]{1,0:T(8,128)(2,1)S(1)}, bf16[384,512]{1,0:T(8,128)(2,1)S(1)}, u32[]{:S(2)}, u32[]{:S(2)}) collective-permute-start(bf16[384,512]{1,0:T(8,128)(2,1)S(1)} %copy-done.17), channel_id=1, source_target_pairs={{0,1},{1,0},{2,3},{3,2},{4,5},{5,4},{6,7},{7,6},{8,9},{9,8},{10,11... | collective-permute-start | bytes 1179656 | tf_op jit(solution)/shard_map/ppermute | solution.py:23
  195.0 8.2 %collective-permute-start.11 = (bf16[192,512]{1,0:T(8,128)(2,1)S(1)}, bf16[192,512]{1,0:T(8,128)(2,1)S(1)}, u32[]{:S(2)}, u32[]{:S(2)}) collective-permute-start(bf16[192,512]{1,0:T(8,128)(2,1)S(1)} %get-tuple-element.95), channel_id=1, source_target_pairs={{0,2},{2,4},{4,6},{6,0},{1,3},{3,5},{5,7},{7,1},{8,10},{10,12},{12... | collective-permute-start | bytes 589832 | tf_op jit(solution)/shard_map/ppermute | solution.py:23
  195.3 7.9 %collective-permute-start.13 = (bf16[192,512]{1,0:T(8,128)(2,1)S(1)}, bf16[192,512]{1,0:T(8,128)(2,1)S(1)}, u32[]{:S(2)}, u32[]{:S(2)}) collective-permute-start(bf16[192,512]{1,0:T(8,128)(2,1)S(1)} %get-tuple-element.96), channel_id=1, source_target_pairs={{0,6},{2,0},{4,2},{6,4},{1,7},{3,1},{5,3},{7,5},{8,14},{10,8},{12,... | collective-permute-start | bytes 589832 | tf_op jit(solution)/shard_map/ppermute | solution.py:23
  204.6 11.0 %collective-permute-start.12 = (bf16[384,512]{1,0:T(8,128)(2,1)S(1)}, bf16[384,512]{1,0:T(8,128)(2,1)S(1)}, u32[]{:S(2)}, u32[]{:S(2)}) collective-permute-start(bf16[384,512]{1,0:T(8,128)(2,1)S(1)} %get-tuple-element.93), channel_id=1, source_target_pairs={{0,2},{2,4},{4,6},{6,0},{1,3},{3,5},{5,7},{7,1},{8,10},{10,12},{12... | collective-permute-start | bytes 1179656 | tf_op jit(solution)/shard_map/ppermute | solution.py:23
  204.7 10.9 %collective-permute-start.14 = (bf16[384,512]{1,0:T(8,128)(2,1)S(1)}, bf16[384,512]{1,0:T(8,128)(2,1)S(1)}, u32[]{:S(2)}, u32[]{:S(2)}) collective-permute-start(bf16[384,512]{1,0:T(8,128)(2,1)S(1)} %get-tuple-element.94), channel_id=1, source_target_pairs={{0,6},{2,0},{4,2},{6,4},{1,7},{3,1},{5,3},{7,5},{8,14},{10,8},{12,... | collective-permute-start | bytes 1179656 | tf_op jit(solution)/shard_map/ppermute | solution.py:23
  (20 other events, 281.4 us)
Sparse Core Ops, SparseCore 0:
  9.9 72.8 all-gather.2
where the time goes:
time: 226 us; the launch traced here: 225 us
  Pallas kernels  67.4 us (30%)
  waiting for transfers between devices  57 us (25%)
  starting transfers between devices  53.8 us (24%)
  blocking collectives  14.6 us (6%)
  between operations  13.8 us (6%)
  local copies, waits for them, and re-layouts  12.5 us (6%)
  other arithmetic  5.45 us (2%)
    ppermute x14, waiting for transfers between devices, shifted(): lax.ppermute(block, axis, [(i, (i + distance) % n) for i in range(n)])  28.4 us
    ppermute x14, starting transfers between devices, shifted(): lax.ppermute(block, axis, [(i, (i + distance) % n) for i in range(n)])  24.1 us
    pallas_call x1, Pallas kernels, project(): pl.pallas_call(functools.partial(proj_kernel, 2, len(blocks)), grid_spec=...  16 us
    pallas_call x3, Pallas kernels, out_partial(): pl.pallas_call(normed_kernel if first else out_kernel, grid_spec=pltpu.Pr...  15.6 us
    all_to_all x1, blocking collectives, local(): packed = lax.all_to_all(packed, 'x', 0, 0, tiled=True)  14.6 us
    pallas_call x2, Pallas kernels, project_gate(): pl.pallas_call(functools.partial(gate_proj_kernel, len(blocks), low), gri...  14.5 us
    all_to_all x1, starting transfers between devices, gathered_weights(): lax.all_to_all(jnp.broadcast_to(edge[None], (peers, *edge.shape)), ('x',...  10.4 us
    all_to_all x1, waiting for transfers between devices, local(): gated = lax.all_to_all(gated, 'x', 0, 0, tiled=True)  7.96 us
  transfers between devices with their start and end apart: 21, of which 9 were waited for; matrix products, arithmetic and copies ran while one was open for 5% of the time, Pallas kernels for 14%

commit v1 on v0

--- a/solution.py
+++ b/solution.py
@@ -472,9 +472,8 @@
     )(at, *inputs, w)
 
 
-def out_shares(gated, gain, w, feats):
+def out_shares(at, gated, gain, w, feats):
     rows = gated.shape[1]
-    at = jnp.stack([lax.axis_index("y"), lax.axis_index("c")])
     far_other, far, normed = out_partial(
         at, ((2, 1), (2, 0)), (gated, gain), w, rows, feats
     )
@@ -556,8 +555,7 @@
     packed = jnp.concatenate(pieces, axis=2).astype(F32) * gain[:, None, None]
     packed = jnp.transpose(packed.astype(BF16), (1, 0, 2))
     packed = lax.all_to_all(packed, "x", 0, 0, tiled=True)
-    place, w_low, w_gate, edges = lax.optimization_barrier(gathered_weights(packed, low, edge))
-    edges = edges.reshape(nx, ny * nc, LEAD, feats)
+    ring = gathered_weights(packed, low, edge)
 
     def own(a):
         size = a.shape[-1] // nx
@@ -569,19 +567,28 @@
     bias_row = jnp.concatenate([own(conv_bias_x), own(conv_bias_bc.reshape(-1))])
     bias_row = row(jnp.pad(bias_row, (0, own_heads + spare)))
     in_lanes = lambda a: row(jnp.pad(own(a), (bc_part, spare)))
+    head = width // heads
+    rows_of = (
+        in_lanes(dt_bias),
+        in_lanes(decay_rate),
+        row(jnp.repeat(own(skip_d), head)),
+        jnp.stack([lax.axis_index("y"), lax.axis_index("c")]),
+    )
+    ring, rows_of = lax.optimization_barrier((ring, rows_of))
+    place, w_low, w_gate, edges = ring
+    dt_bias_row, rate_row, skip_row, at = rows_of
+    edges = edges.reshape(nx, ny * nc, LEAD, feats)
     x_conv, quarter, dt = project(
-        place, edges, gathered, w_low, tap_rows, bias_row, in_lanes(dt_bias), part, bc_part
-    )
-    head = width // heads
+        place, edges, gathered, w_low, tap_rows, bias_row, dt_bias_row, part, bc_part
+    )
     half = nx // 2
     quarters, (cum, scaled), early_gate = lax.optimization_barrier(
         (
             lax.all_to_all(quarter, "x", 0, 0, tiled=True),
-            block_decays(x_conv, dt, in_lanes(decay_rate), bc_part, head),
+            block_decays(x_conv, dt, rate_row, bc_part, head),
             project_gate(place, gathered, w_gate, dt, low, 0, half),
         )
     )
-    skip_row = row(jnp.repeat(own(skip_d), head))
     enter, message = block_states(scaled, quarters, cum, bc_part, head, nz)
     received, (y, c_rows) = lax.optimization_barrier(
         (
@@ -601,7 +608,7 @@
     gated = gate_blocks(y, cum, c_rows, enter, entering, gates, bc_part, head)
     gated = lax.all_to_all(gated, "x", 0, 0, tiled=True)
 
-    summed = out_shares(gated, row(out_gain), w_out, feats)
+    summed = out_shares(at, gated, row(out_gain), w_out, feats)
     return (hidden_in.astype(F32) + summed).astype(BF16)
 
 

time: 226 us -> 225 us (level)
  blocking collectives: 14.6 us -> 27.6 us
  waiting for transfers between devices: 57 us -> 48.4 us
  starting transfers between devices: 53.8 us -> 49.8 us
    all_to_all x0 -> x1, blocking collectives: none -> 12.9 us  [local(): gated = lax.all_to_all(gated, 'x', 0, 0, tiled=True)]
    all_to_all x1 -> x0, waiting for transfers between devices: 7.96 us -> none  [local(): gated = lax.all_to_all(gated, 'x', 0, 0, tiled=True)]
    all_to_all x1 -> x0, starting transfers between devices: 4.13 us -> none  [local(): gated = lax.all_to_all(gated, 'x', 0, 0, tiled=True)]
    unnamed x49 -> x47, local copies, waits for them, and re-layouts: 4.69 us -> 3.77 us
  transfers between devices with their start and end apart: 21 -> 20, of which waited for: 9 -> 8; matrix products, arithmetic and copies ran while one was open for 5% -> 5% of each run, Pallas kernels for 14% -> 14%
where the time goes in v1:
time: 225 us; the launch traced here: 223 us
  Pallas kernels  67.5 us (30%)
  starting transfers between devices  49.8 us (22%)
  waiting for transfers between devices  48.4 us (22%)
  blocking collectives  27.6 us (12%)
  between operations  13.7 us (6%)
  local copies, waits for them, and re-layouts  11 us (5%)
  other arithmetic  5.46 us (2%)
    ppermute x14, waiting for transfers between devices, shifted(): lax.ppermute(block, axis, [(i, (i + distance) % n) for i in range(n)])  28.4 us
    ppermute x14, starting transfers between devices, shifted(): lax.ppermute(block, axis, [(i, (i + distance) % n) for i in range(n)])  24.3 us
    pallas_call x1, Pallas kernels, project(): pl.pallas_call(functools.partial(proj_kernel, 2, len(blocks)), grid_spec=...  16 us
    pallas_call x3, Pallas kernels, out_partial(): pl.pallas_call(normed_kernel if first else out_kernel, grid_spec=pltpu.Pr...  15.6 us
    all_to_all x1, blocking collectives, local(): packed = lax.all_to_all(packed, 'x', 0, 0, tiled=True)  14.6 us
    pallas_call x2, Pallas kernels, project_gate(): pl.pallas_call(functools.partial(gate_proj_kernel, len(blocks), low), gri...  14.5 us
    all_to_all x1, blocking collectives, local(): gated = lax.all_to_all(gated, 'x', 0, 0, tiled=True)  12.9 us
    all_to_all x1, starting transfers between devices, gathered_weights(): lax.all_to_all(jnp.broadcast_to(edge[None], (peers, *edge.shape)), ('x',...  10.4 us
  transfers between devices with their start and end apart: 20, of which 8 were waited for; matrix products, arithmetic and copies ran while one was open for 5% of the time, Pallas kernels for 14%

profile of v1, /device:TPU:1, one launch (start us, length us, event | category | flops | bytes accessed | tf_op | source)
XLA Modules:
  0.0 223.4 jit_solution(5702819437502681770)
XLA Ops:
  10.8 14.6 %all_to_all.30.refs_0_ = bf16[4,128,640]{2,1,0:T(8,128)(2,1)S(1)} all-to-all(bf16[4,128,640]{2,1,0:T(8,128)(2,1)S(1)} %fusion.5), channel_id=1, replica_groups=mesh['x'=4,'z'=8,'y'=4,'c'=2] {'x'}, dimensions={0} | all-to-all | bytes 1310720 | tf_op jit(solution)/shard_map/all_to_all | solution.py:557
  27.1 3.9 %collective-permute-start.1 = (bf16[4,128,640]{2,1,0:T(8,128)(2,1)S(1)}, bf16[4,128,640]{2,1,0:T(8,128)(2,1)S(1)}, u32[]{:S(2)}, u32[]{:S(2)}) collective-permute-start(bf16[4,128,640]{2,1,0:T(8,128)(2,1)S(1)} %all_to_all.30.refs_0_), channel_id=1, source_target_pairs={{0,56},{8,0},{16,8},{24,16},{32,24},{40,32},{48,40},{56,48},{1,57}... | collective-permute-start | bytes 1966088 | tf_op jit(solution)/shard_map/ppermute | solution.py:23
  33.0 6.7 %collective-permute-done.2 = bf16[16,512]{1,0:T(8,128)(2,1)S(1)} collective-permute-done((bf16[16,512]{1,0:T(8,128)(2,1)S(1)}, bf16[16,512]{1,0:T(8,128)(2,1)S(1)}, u32[]{:S(2)}, u32[]{:S(2)}) %collective-permute-start.2) | collective-permute-done | bytes 16416 | tf_op jit(solution)/shard_map/ppermute | solution.py:549
  39.7 4.6 %collective-permute-done.refs_1_ = bf16[4,128,640]{2,1,0:T(8,128)(2,1)S(1)} collective-permute-done((bf16[4,128,640]{2,1,0:T(8,128)(2,1)S(1)}, bf16[4,128,640]{2,1,0:T(8,128)(2,1)S(1)}, u32[]{:S(2)}, u32[]{:S(2)}) %collective-permute-start) | collective-permute-done | bytes 655392 | tf_op jit(solution)/shard_map/ppermute | solution.py:23
  47.1 12.4 %collective-permute-done.3.refs_3_ = bf16[4,128,640]{2,1,0:T(8,128)(2,1)} collective-permute-done((bf16[4,128,640]{2,1,0:T(8,128)(2,1)S(1)}, bf16[4,128,640]{2,1,0:T(8,128)(2,1)}, u32[]{:S(2)}, u32[]{:S(2)}) %collective-permute-start.3) | collective-permute-done | bytes 655392 | tf_op jit(solution)/shard_map/ppermute | solution.py:23
  64.6 10.4 %all-to-all-start.1 = ((bf16[32,16,512]{2,1,0:T(8,128)(2,1)}), bf16[32,16,512]{2,1,0:T(8,128)(2,1)}, u32[]{:S(2)}, u32[]{:S(2)}) async-start(bf16[32,16,512]{2,1,0:T(8,128)(2,1)} %broadcast_in_dim.7), calls=%async_computation.1 | async-start | bytes 1048576 | tf_op jit(solution)/shard_map/all_to_all | solution.py:510
  81.2 5.9 %all-to-all-done.1 = bf16[32,16,512]{2,1,0:T(8,128)(2,1)} async-done(((bf16[32,16,512]{2,1,0:T(8,128)(2,1)}), bf16[32,16,512]{2,1,0:T(8,128)(2,1)}, u32[]{:S(2)}, u32[]{:S(2)}) %all-to-all-start.1) | async-done | bytes 524320 | tf_op jit(solution)/shard_map/all_to_all | solution.py:510
  87.8 16.0 %project.1 = (bf16[4,384,256]{2,1,0:T(8,128)(2,1)}, bf16[4,2,384,128]{3,2,1,0:T(8,128)(2,1)}, f32[4,384,128]{2,1,0:T(8,128)}) custom-call(s32[8]{0:T(128)} %compare_select_fusion.place_ref, bf16[4,8,16,512]{3,2,1,0:T(8,128)(2,1)} %bitcast.10.edge_ref, bf16[4,8,384,512]{3,2,1,0:T(8,128)(2,1)} %bitcast.35, bf16[4,128,640]{2,1,0:T(8,128)(2,1)} %copy-done.1, ...), custom_call_target="tpu_custom_call" | custom-call | flops 4831838208 | bytes 12582912 | tf_op jit(solution)/shard_map/project/pallas_call | solution.py:123
  103.8 3.7 %all-to-all-start.2 = ((bf16[4,2,384,128]{3,2,1,0:T(8,128)(2,1)}), bf16[4,2,384,128]{3,2,1,0:T(8,128)(2,1)S(1)}, u32[]{:S(2)}, u32[]{:S(2)}) async-start(bf16[4,2,384,128]{3,2,1,0:T(8,128)(2,1)} %get-tuple-element.68), calls=%async_computation.2 | async-start | bytes 1572864 | tf_op jit(solution)/shard_map/all_to_all | solution.py:587
  107.5 4.4 %block_decays.1 = (f32[4,384,128]{2,1,0:T(8,128)}, bf16[4,384,256]{2,1,0:T(8,128)(2,1)}) custom-call(bf16[4,384,256]{2,1,0:T(8,128)(2,1)} %get-tuple-element.69.x_ref, f32[4,384,128]{2,1,0:T(8,128)} %get-tuple-element.70.dt_ref.refs_8_, f32[1,128]{1,0:T(1,128)} %get-tuple-element.71.rate_ref), custom_call_target="tpu_custom_call" | custom-call | flops 402653184 | bytes 3145728 | tf_op jit(solution)/shard_map/block_decays/pallas_call | solution.py:233
  111.9 7.3 %project_gate.2.z0_ref = bf16[2,384,256]{2,1,0:T(8,128)(2,1)} custom-call(s32[8]{0:T(128)} %compare_select_fusion.place_ref, bf16[4,8,384,512]{3,2,1,0:T(8,128)(2,1)} %bitcast.36, bf16[4,128,640]{2,1,0:T(8,128)(2,1)} %copy-done.1, bf16[4,128,640]{2,1,0:T(8,128)(2,1)} %copy-done.4, bf16[4,128,640]{2,1,0:T(8,128)(2,1)} %copy-done.5, ...), custom_call_target="tpu_custom_call" | custom-call | flops 1610612736 | bytes 12582912 | tf_op jit(solution)/shard_map/project_gate/pallas_call | solution.py:178
  120.1 4.5 %block_states.1 = (f32[4,2,128,256]{3,2,1,0:T(8,128)}, bf16[8,72,256]{2,1,0:T(8,128)(2,1)}) custom-call(bf16[4,384,256]{2,1,0:T(8,128)(2,1)} %get-tuple-element.82.scaled_ref, bf16[4,2,384,128]{3,2,1,0:T(8,128)(2,1)} %copy-done.6, f32[4,384,128]{2,1,0:T(8,128)} %get-tuple-element.84.cum_ref), custom_call_target="tpu_custom_call" | custom-call | flops 100663296 | bytes 2621440 | tf_op jit(solution)/shard_map/block_states/pallas_call | solution.py:293
  124.5 6.7 %all-to-all-start.3 = ((bf16[8,72,256]{2,1,0:T(8,128)(2,1)}), bf16[8,72,256]{2,1,0:T(8,128)(2,1)S(1)}, u32[]{:S(2)}, u32[]{:S(2)}) async-start(bf16[8,72,256]{2,1,0:T(8,128)(2,1)} %get-tuple-element.85), calls=%async_computation.3 | async-start | bytes 589824 | tf_op jit(solution)/shard_map/all_to_all | solution.py:595
  131.3 6.1 %intra_blocks.1 = (f32[4,384,256]{2,1,0:T(8,128)}, bf16[4,384,128]{2,1,0:T(8,128)(2,1)}) custom-call(bf16[4,384,256]{2,1,0:T(8,128)(2,1)} %get-tuple-element.69.x_ref, bf16[4,2,384,128]{3,2,1,0:T(8,128)(2,1)} %copy-done.6, f32[4,384,128]{2,1,0:T(8,128)} %get-tuple-element.70.dt_ref.refs_8_, f32[4,384,128]{2,1,0:T(8,128)} %get-tuple-element.84.cum_ref, ...), custom_call_target="tpu_custom_call" | custom-call | flops 3221225472 | bytes 3932160 | tf_op jit(solution)/shard_map/intra_blocks/pallas_call | solution.py:333
  137.3 4.6 %all-to-all-done.3.r_ref = bf16[8,72,256]{2,1,0:T(8,128)(2,1)S(1)} async-done(((bf16[8,72,256]{2,1,0:T(8,128)(2,1)}), bf16[8,72,256]{2,1,0:T(8,128)(2,1)S(1)}, u32[]{:S(2)}, u32[]{:S(2)}) %all-to-all-start.3) | async-done | bytes 294944 | tf_op jit(solution)/shard_map/all_to_all | solution.py:595
  144.4 3.4 %all-to-all-start.4 = ((bf16[8,64,256]{2,1,0:T(8,128)(2,1)}), bf16[8,64,256]{2,1,0:T(8,128)(2,1)S(1)}, u32[]{:S(2)}, u32[]{:S(2)}) async-start(bf16[8,64,256]{2,1,0:T(8,128)(2,1)} %combine_states.1), calls=%async_computation.4 | async-start | bytes 524288 | tf_op jit(solution)/shard_map/all_to_all | solution.py:603
  147.8 7.3 %project_gate.3.z1_ref = bf16[2,384,256]{2,1,0:T(8,128)(2,1)} custom-call(s32[8]{0:T(128)} %compare_select_fusion.place_ref, bf16[4,8,384,512]{3,2,1,0:T(8,128)(2,1)} %bitcast.37, bf16[4,128,640]{2,1,0:T(8,128)(2,1)} %copy-done.1, bf16[4,128,640]{2,1,0:T(8,128)(2,1)} %copy-done.4, bf16[4,128,640]{2,1,0:T(8,128)(2,1)} %copy-done.5, ...), custom_call_target="tpu_custom_call" | custom-call | flops 1610612736 | bytes 12582912 | tf_op jit(solution)/shard_map/project_gate/pallas_call | solution.py:178
  157.8 4.6 %gate_blocks.1 = bf16[4,384,256]{2,1,0:T(8,128)(2,1)} custom-call(f32[4,384,256]{2,1,0:T(8,128)} %get-tuple-element.89.y_ref, f32[4,384,128]{2,1,0:T(8,128)} %get-tuple-element.84.cum_ref, bf16[4,384,128]{2,1,0:T(8,128)(2,1)} %get-tuple-element.90.c_ref, f32[4,2,128,256]{3,2,1,0:T(8,128)} %get-tuple-element.91.enter_ref, bf16[8,64,256]{2,1,0:T(8,128)(2,1)} %copy-done.10, ...), custom_call_target="tpu_custom_call" | custom-call | flops 100663296 | bytes 5373952 | tf_op jit(solution)/shard_map/gate_blocks/pallas_call | solution.py:395
  162.5 12.9 %all_to_all.31.g_ref = bf16[4,384,256]{2,1,0:T(8,128)(2,1)} all-to-all(bf16[4,384,256]{2,1,0:T(8,128)(2,1)} %gate_blocks.1), channel_id=1, replica_groups=mesh['x'=4,'z'=8,'y'=4,'c'=2] {'x'}, dimensions={0} | all-to-all | bytes 1572864 | tf_op jit(solution)/shard_map/all_to_all | solution.py:609
  175.4 4.6 %out_normed.1 = (bf16[384,512]{1,0:T(8,128)(2,1)}, bf16[384,512]{1,0:T(8,128)(2,1)}, bf16[384,1024]{1,0:T(8,128)(2,1)}) custom-call(s32[2]{0:T(128)} %pad_add_fusion.at_ref, bf16[4,384,256]{2,1,0:T(8,128)(2,1)} %all_to_all.31.g_ref, f32[1,1024]{1,0:T(1,128)} %bitcast.42, bf16[1024,4096]{1,0:T(8,128)(2,1)} %w_ref.5), custom_call_target="tpu_custom_call" | custom-call | flops 805306368 | bytes 1572864 | tf_op jit(solution)/shard_map/out_normed/pallas_call | solution.py:458
  180.0 5.6 %out_partial.3 = bf16[3,384,512]{2,1,0:T(8,128)(2,1)} custom-call(s32[2]{0:T(128)} %pad_add_fusion.at_ref, bf16[384,1024]{1,0:T(8,128)(2,1)} %get-tuple-element.98.normed_ref, bf16[1024,4096]{1,0:T(8,128)(2,1)} %w_ref.5), custom_call_target="tpu_custom_call" | custom-call | flops 1207959552 | bytes 1966080 | tf_op jit(solution)/shard_map/out_partial/pallas_call | solution.py:458
  185.6 4.9 %collective-permute-start.9 = (bf16[3,384,512]{2,1,0:T(8,128)(2,1)}, bf16[3,384,512]{2,1,0:T(8,128)(2,1)S(1)}, u32[]{:S(2)}, u32[]{:S(2)}) collective-permute-start(bf16[3,384,512]{2,1,0:T(8,128)(2,1)} %out_partial.3), channel_id=1, source_target_pairs={{0,1},{1,0},{2,3},{3,2},{4,5},{5,4},{6,7},{7,6},{8,9},{9,8},{10,11... | collective-permute-start | bytes 3538952 | tf_op jit(solution)/shard_map/ppermute | solution.py:23
  196.6 5.4 %out_partial.2 = bf16[3,384,512]{2,1,0:T(8,128)(2,1)} custom-call(s32[2]{0:T(128)} %pad_add_fusion.at_ref, bf16[384,1024]{1,0:T(8,128)(2,1)} %get-tuple-element.98.normed_ref, bf16[1024,4096]{1,0:T(8,128)(2,1)} %w_ref.5), custom_call_target="tpu_custom_call" | custom-call | flops 1207959552 | bytes 1966080 | tf_op jit(solution)/shard_map/out_partial/pallas_call | solution.py:458
  206.3 8.3 %collective-permute-done.12 = bf16[384,512]{1,0:T(8,128)(2,1)S(1)} collective-permute-done((bf16[384,512]{1,0:T(8,128)(2,1)S(1)}, bf16[384,512]{1,0:T(8,128)(2,1)S(1)}, u32[]{:S(2)}, u32[]{:S(2)}) %collective-permute-start.12) | collective-permute-done | bytes 393248 | tf_op jit(solution)/shard_map/ppermute | solution.py:23
  (107 shorter events, 40.8 us)
Async XLA Ops:
  6.5 56.7 %copy-start = (f32[4,1024]{1,0:T(4,128)S(1)}, f32[4,1024]{1,0:T(4,128)}, u32[]{:S(2)}) copy-start(f32[4,1024]{1,0:T(4,128)} %param.24) | copy-start | bytes 49156
  6.5 81.3 %all-gather.3.cloned.1.call-start = ((), (), s32[]{:S(2)}) async-start(), calls=%async_computation.6 | async-start | bytes 12976128 | tf_op jit(solution)/shard_map/all_gather | solution.py:546
  10.6 52.5 %copy-start.17 = (f32[1,256]{1,0:T(1,128)S(1)}, f32[1,256]{1,0:T(1,128)}, u32[]{:S(2)}) copy-start(f32[1,256]{1,0:T(1,128)} %param.27) | copy-start | bytes 3076
  10.6 52.5 %copy-start.15 = (f32[4,1,256]{2,1,0:T(1,128)S(1)}, f32[4,1,256]{2,1,0:T(1,128)}, u32[]{:S(2)}) copy-start(f32[4,1,256]{2,1,0:T(1,128)} %param.25) | copy-start | bytes 12292
  25.4 50.5 %copy-start.1 = (bf16[4,128,640]{2,1,0:T(8,128)(2,1)}, bf16[4,128,640]{2,1,0:T(8,128)(2,1)S(1)}, u32[]{:S(2)}) copy-start(bf16[4,128,640]{2,1,0:T(8,128)(2,1)S(1)} %all_to_all.30.refs_0_) | copy-start | bytes 1966084
  25.4 18.9 %collective-permute-start = (bf16[4,128,640]{2,1,0:T(8,128)(2,1)S(1)}, bf16[4,128,640]{2,1,0:T(8,128)(2,1)S(1)}, u32[]{:S(2)}, u32[]{:S(2)}) collective-permute-start(bf16[4,128,640]{2,1,0:T(8,128)(2,1)S(1)} %all_to_all.30.refs_0_), channel_id=1, source_target_pairs={{0,8},{8,16},{16,24},{24,32},{32,40},{40,48},{48,56},{56,0},{1,9},... | collective-permute-start | bytes 1966088 | tf_op jit(solution)/shard_map/ppermute | solution.py:23
  27.1 17.2 %collective-permute-start.1 = (bf16[4,128,640]{2,1,0:T(8,128)(2,1)S(1)}, bf16[4,128,640]{2,1,0:T(8,128)(2,1)S(1)}, u32[]{:S(2)}, u32[]{:S(2)}) collective-permute-start(bf16[4,128,640]{2,1,0:T(8,128)(2,1)S(1)} %all_to_all.30.refs_0_), channel_id=1, source_target_pairs={{0,56},{8,0},{16,8},{24,16},{32,24},{40,32},{48,40},{56,48},{1,57}... | collective-permute-start | bytes 1966088 | tf_op jit(solution)/shard_map/ppermute | solution.py:23
  31.7 8.0 %collective-permute-start.2 = (bf16[16,512]{1,0:T(8,128)(2,1)S(1)}, bf16[16,512]{1,0:T(8,128)(2,1)S(1)}, u32[]{:S(2)}, u32[]{:S(2)}) collective-permute-start(bf16[16,512]{1,0:T(8,128)(2,1)S(1)} %slice.15), channel_id=1, source_target_pairs={{0,8},{8,16},{16,24},{24,32},{32,40},{40,48},{48,56},{56,64},{64,7... | collective-permute-start | bytes 49160 | tf_op jit(solution)/shard_map/ppermute | solution.py:549
  44.3 15.1 %collective-permute-start.3 = (bf16[4,128,640]{2,1,0:T(8,128)(2,1)S(1)}, bf16[4,128,640]{2,1,0:T(8,128)(2,1)}, u32[]{:S(2)}, u32[]{:S(2)}) collective-permute-start(bf16[4,128,640]{2,1,0:T(8,128)(2,1)S(1)} %collective-permute-done.refs_1_), channel_id=1, source_target_pairs={{0,8},{8,16},{16,24},{24,32},{32,40},{40,48},{48,56},{56,0},{1,9},... | collective-permute-start | bytes 1966088 | tf_op jit(solution)/shard_map/ppermute | solution.py:23
  44.4 16.0 %collective-permute-start.4 = (bf16[4,128,640]{2,1,0:T(8,128)(2,1)S(1)}, bf16[4,128,640]{2,1,0:T(8,128)(2,1)}, u32[]{:S(2)}, u32[]{:S(2)}) collective-permute-start(bf16[4,128,640]{2,1,0:T(8,128)(2,1)S(1)} %collective-permute-done.1.refs_2_), channel_id=1, source_target_pairs={{0,56},{8,0},{16,8},{24,16},{32,24},{40,32},{48,40},{56,48},{1,57}... | collective-permute-start | bytes 1966088 | tf_op jit(solution)/shard_map/ppermute | solution.py:23
  59.4 15.6 %collective-permute-start.5 = (bf16[4,128,640]{2,1,0:T(8,128)(2,1)}, bf16[4,128,640]{2,1,0:T(8,128)(2,1)S(1)}, u32[]{:S(2)}, u32[]{:S(2)}) collective-permute-start(bf16[4,128,640]{2,1,0:T(8,128)(2,1)} %collective-permute-done.3.refs_3_), channel_id=1, source_target_pairs={{0,8},{8,16},{16,24},{24,32},{32,40},{40,48},{48,56},{56,0},{1,9},... | collective-permute-start | bytes 1966088 | tf_op jit(solution)/shard_map/ppermute | solution.py:23
  60.4 16.2 %collective-permute-start.6 = (bf16[4,128,640]{2,1,0:T(8,128)(2,1)}, bf16[4,128,640]{2,1,0:T(8,128)(2,1)S(1)}, u32[]{:S(2)}, u32[]{:S(2)}) collective-permute-start(bf16[4,128,640]{2,1,0:T(8,128)(2,1)} %collective-permute-done.4.refs_4_), channel_id=1, source_target_pairs={{0,56},{8,0},{16,8},{24,16},{32,24},{40,32},{48,40},{56,48},{1,57}... | collective-permute-start | bytes 1966088 | tf_op jit(solution)/shard_map/ppermute | solution.py:23
  64.6 22.5 %all-to-all-start.1 = ((bf16[32,16,512]{2,1,0:T(8,128)(2,1)}), bf16[32,16,512]{2,1,0:T(8,128)(2,1)}, u32[]{:S(2)}, u32[]{:S(2)}) async-start(bf16[32,16,512]{2,1,0:T(8,128)(2,1)} %broadcast_in_dim.7), calls=%async_computation.1 | async-start | bytes 1048576 | tf_op jit(solution)/shard_map/all_to_all | solution.py:510
  75.9 11.2 %collective-permute-start.7 = (bf16[4,128,384]{2,1,0:T(8,128)(2,1)}, bf16[4,128,384]{2,1,0:T(8,128)(2,1)}, u32[]{:S(2)}, u32[]{:S(2)}) collective-permute-start(bf16[4,128,384]{2,1,0:T(8,128)(2,1)} %slice.20), channel_id=1, source_target_pairs={{0,8},{8,16},{16,24},{24,32},{32,40},{40,48},{48,56},{56,0},{1,9},... | collective-permute-start | bytes 1179656 | tf_op jit(solution)/shard_map/ppermute | solution.py:23
  76.6 10.5 %collective-permute-start.8 = (bf16[4,128,256]{2,1,0:T(8,128)(2,1)S(1)}, bf16[4,128,256]{2,1,0:T(8,128)(2,1)S(1)}, u32[]{:S(2)}, u32[]{:S(2)}) collective-permute-start(bf16[4,128,256]{2,1,0:T(8,128)(2,1)S(1)} %slice.21), channel_id=1, source_target_pairs={{0,56},{8,0},{16,8},{24,16},{32,24},{40,32},{48,40},{56,48},{1,57}... | collective-permute-start | bytes 786440 | tf_op jit(solution)/shard_map/ppermute | solution.py:23
  103.8 15.4 %all-to-all-start.2 = ((bf16[4,2,384,128]{3,2,1,0:T(8,128)(2,1)}), bf16[4,2,384,128]{3,2,1,0:T(8,128)(2,1)S(1)}, u32[]{:S(2)}, u32[]{:S(2)}) async-start(bf16[4,2,384,128]{3,2,1,0:T(8,128)(2,1)} %get-tuple-element.68), calls=%async_computation.2 | async-start | bytes 1572864 | tf_op jit(solution)/shard_map/all_to_all | solution.py:587
  124.5 17.4 %all-to-all-start.3 = ((bf16[8,72,256]{2,1,0:T(8,128)(2,1)}), bf16[8,72,256]{2,1,0:T(8,128)(2,1)S(1)}, u32[]{:S(2)}, u32[]{:S(2)}) async-start(bf16[8,72,256]{2,1,0:T(8,128)(2,1)} %get-tuple-element.85), calls=%async_computation.3 | async-start | bytes 589824 | tf_op jit(solution)/shard_map/all_to_all | solution.py:595
  144.4 12.7 %all-to-all-start.4 = ((bf16[8,64,256]{2,1,0:T(8,128)(2,1)}), bf16[8,64,256]{2,1,0:T(8,128)(2,1)S(1)}, u32[]{:S(2)}, u32[]{:S(2)}) async-start(bf16[8,64,256]{2,1,0:T(8,128)(2,1)} %combine_states.1), calls=%async_computation.4 | async-start | bytes 524288 | tf_op jit(solution)/shard_map/all_to_all | solution.py:603
  185.6 16.5 %collective-permute-start.9 = (bf16[3,384,512]{2,1,0:T(8,128)(2,1)}, bf16[3,384,512]{2,1,0:T(8,128)(2,1)S(1)}, u32[]{:S(2)}, u32[]{:S(2)}) collective-permute-start(bf16[3,384,512]{2,1,0:T(8,128)(2,1)} %out_partial.3), channel_id=1, source_target_pairs={{0,1},{1,0},{2,3},{3,2},{4,5},{5,4},{6,7},{7,6},{8,9},{9,8},{10,11... | collective-permute-start | bytes 3538952 | tf_op jit(solution)/shard_map/ppermute | solution.py:23
  190.5 3.2 %collective-permute-start.10 = (bf16[384,512]{1,0:T(8,128)(2,1)S(1)}, bf16[384,512]{1,0:T(8,128)(2,1)S(1)}, u32[]{:S(2)}, u32[]{:S(2)}) collective-permute-start(bf16[384,512]{1,0:T(8,128)(2,1)S(1)} %copy-done.16), channel_id=1, source_target_pairs={{0,1},{1,0},{2,3},{3,2},{4,5},{5,4},{6,7},{7,6},{8,9},{9,8},{10,11... | collective-permute-start | bytes 1179656 | tf_op jit(solution)/shard_map/ppermute | solution.py:23
  193.9 8.2 %collective-permute-start.11 = (bf16[192,512]{1,0:T(8,128)(2,1)S(1)}, bf16[192,512]{1,0:T(8,128)(2,1)S(1)}, u32[]{:S(2)}, u32[]{:S(2)}) collective-permute-start(bf16[192,512]{1,0:T(8,128)(2,1)S(1)} %get-tuple-element.103), channel_id=1, source_target_pairs={{0,2},{2,4},{4,6},{6,0},{1,3},{3,5},{5,7},{7,1},{8,10},{10,12},{12... | collective-permute-start | bytes 589832 | tf_op jit(solution)/shard_map/ppermute | solution.py:23
  194.0 8.1 %collective-permute-start.13 = (bf16[192,512]{1,0:T(8,128)(2,1)S(1)}, bf16[192,512]{1,0:T(8,128)(2,1)S(1)}, u32[]{:S(2)}, u32[]{:S(2)}) collective-permute-start(bf16[192,512]{1,0:T(8,128)(2,1)S(1)} %get-tuple-element.104), channel_id=1, source_target_pairs={{0,6},{2,0},{4,2},{6,4},{1,7},{3,1},{5,3},{7,5},{8,14},{10,8},{12,... | collective-permute-start | bytes 589832 | tf_op jit(solution)/shard_map/ppermute | solution.py:23
  203.5 11.0 %collective-permute-start.12 = (bf16[384,512]{1,0:T(8,128)(2,1)S(1)}, bf16[384,512]{1,0:T(8,128)(2,1)S(1)}, u32[]{:S(2)}, u32[]{:S(2)}) collective-permute-start(bf16[384,512]{1,0:T(8,128)(2,1)S(1)} %get-tuple-element.101), channel_id=1, source_target_pairs={{0,2},{2,4},{4,6},{6,0},{1,3},{3,5},{5,7},{7,1},{8,10},{10,12},{12... | collective-permute-start | bytes 1179656 | tf_op jit(solution)/shard_map/ppermute | solution.py:23
  203.6 10.9 %collective-permute-start.14 = (bf16[384,512]{1,0:T(8,128)(2,1)S(1)}, bf16[384,512]{1,0:T(8,128)(2,1)S(1)}, u32[]{:S(2)}, u32[]{:S(2)}) collective-permute-start(bf16[384,512]{1,0:T(8,128)(2,1)S(1)} %get-tuple-element.102), channel_id=1, source_target_pairs={{0,6},{2,0},{4,2},{6,4},{1,7},{3,1},{5,3},{7,5},{8,14},{10,8},{12,... | collective-permute-start | bytes 1179656 | tf_op jit(solution)/shard_map/ppermute | solution.py:23
  (18 other events, 278.4 us)
Sparse Core Ops, SparseCore 0:
  9.9 72.7 all-gather.2
